TPU v7x, 32 devices: a whole 2x2x4 slice. The times are simulated.
32 devices in a mesh: blk: 16 (over z, y, x), ch: 2 (over core).
Axes of the slice: x: 2, y: 2, z: 4, core: 2. Of those that a mesh axis runs over, the one named last changes fastest.
Arguments:
- features: bfloat16 [4096, 128], P('blk'), may hold values from -6 to 6
- out_grad: bfloat16 [4096, 256], P('blk', 'ch'), may hold values from -6 to 6
- weight: bfloat16 [256, 256], P('ch'), may hold values from -0.375 to 0.375
- neighbour_slot: int32 [4096, 20], P('blk'), may hold values from 0 to 2303
- argmax_edge: int32 [4096, 256], P('blk', 'ch'), may hold values from 0 to 19
Outputs:
- feature_grad: float32 [4096, 128], P('blk')
- weight_grad: float32 [256, 256], P('ch')
Inputs may be any that keep to these rules, and one draw needn't show every extreme that they name: `neighbour_slot`: slot s stands for row s mod 256 of the block s // 256 - 4 places away from the point's own block around the cycle.
All inputs are finite; a program needn't handle non-finite values.
Results may differ from a plain program's by a relative error of at most 0.0044.
Values may be sent and summed in bfloat16 or wider, within the bound.
No kernel may reach another device: no remote copies, remote signals or barrier semaphores. Data moves between devices by JAX's collectives and lax.ppermute only.
A program may use at most 64 MiB of HBM per device.

v0:
```python
import jax
import jax.numpy as jnp
from jax import lax
from jax.sharding import PartitionSpec as P

REACH = 4


def shifted(block, axis, distance):
    devices = range(lax.axis_size(axis))
    route = [((i - distance) % len(devices), i) for i in devices]
    return lax.ppermute(block, axis, route)


def silu_slope(pre):
    sig = jax.nn.sigmoid(pre)
    return sig * (1.0 + pre * (1.0 - sig))


def fetch_blocks(piece):
    fetched = []
    for offset in range(-REACH, REACH + 1):
        if offset != 0:
            fetched.append(shifted(piece, "blk", -offset))
    return fetched


def deliver_blocks(stacked):
    summed_all = stacked[REACH]
    for position in range(2 * REACH + 1):
        if position != REACH:
            summed_all = summed_all + shifted(stacked[position], "blk", position - REACH)
    return summed_all


def on_device(features, out_grad, weight, neighbour_slot, argmax_edge):
    points = features.shape[0]
    in_width = features.shape[1]
    columns = weight.shape[0]
    neighbours = neighbour_slot.shape[1]
    w_self = weight[:, :in_width]
    w_nbr = weight[:, in_width:]
    w_diff = (w_self.astype(jnp.float32) - w_nbr.astype(jnp.float32)).astype(jnp.bfloat16)
    remote_list = fetch_blocks(features)
    window = jnp.concatenate(remote_list[:REACH] + [features] + remote_list[REACH:], axis=0)
    window_rows = window.shape[0]
    self_term = jnp.dot(features, w_diff.T, preferred_element_type=jnp.float32)
    w_nbr_t = w_nbr.T
    block_rows = min(256, points)
    block_count = points // block_rows
    window_ids = jnp.arange(window_rows, dtype=jnp.int32)
    edge_order = jnp.arange(neighbours, dtype=jnp.int32)

    def point_block(window_acc, inputs):
        self_rows, slot_rows, grad_rows, pick_rows = inputs
        grad_float = grad_rows.astype(jnp.float32)

        def per_edge(carry, edge_index):
            acc_window, edge_total = carry
            slot_col = lax.dynamic_slice_in_dim(slot_rows, edge_index, 1, 1)
            one_hot = (slot_col == window_ids[None, :]).astype(jnp.bfloat16)
            picked = jnp.dot(one_hot, window, preferred_element_type=jnp.float32).astype(
                jnp.bfloat16
            )
            pre = self_rows + jnp.dot(picked, w_nbr_t, preferred_element_type=jnp.float32)
            keep = pick_rows == edge_index
            edge_grad = jnp.where(keep, grad_float * silu_slope(pre), 0.0).astype(jnp.bfloat16)
            edge_total = edge_total + edge_grad.astype(jnp.float32)
            acc_window = acc_window + lax.dot_general(
                one_hot, edge_grad, (((0,), (0,)), ((), ())), preferred_element_type=jnp.float32
            )
            return ((acc_window, edge_total), None)

        start_total = jnp.zeros((self_rows.shape[0], columns), jnp.float32)
        (window_acc, edge_total), _ = lax.scan(per_edge, (window_acc, start_total), edge_order)
        return (window_acc, edge_total.astype(jnp.bfloat16))

    start_window = jnp.zeros((window_rows, columns), jnp.float32)
    gathered_float, grad_sum = lax.scan(
        point_block,
        start_window,
        (
            self_term.reshape(block_count, block_rows, columns),
            neighbour_slot.reshape(block_count, block_rows, neighbours),
            out_grad.reshape(block_count, block_rows, columns),
            argmax_edge.reshape(block_count, block_rows, columns),
        ),
    )
    gathered = gathered_float.astype(jnp.bfloat16)
    grad_sum = grad_sum.reshape(points, columns)
    own_part = lax.dot_general(
        grad_sum, features, (((0,), (0,)), ((), ())), preferred_element_type=jnp.float32
    )
    nbr_total = lax.dot_general(
        gathered, window, (((0,), (0,)), ((), ())), preferred_element_type=jnp.float32
    )
    weight_terms = jnp.concatenate([own_part, nbr_total - own_part], axis=1)
    total_points = points * lax.axis_size("blk")
    weight_grad = lax.psum(weight_terms, "blk") * total_points ** (-0.5)
    self_grad = jnp.dot(grad_sum, w_diff, preferred_element_type=jnp.float32)
    contrib = jnp.dot(gathered, w_nbr, preferred_element_type=jnp.float32)
    contrib = contrib.reshape(2 * REACH + 1, points, in_width)
    contrib = contrib.at[REACH].add(self_grad)
    summed = deliver_blocks(contrib)
    feature_grad = lax.psum(summed, "ch")
    return (feature_grad, weight_grad)


def solution(mesh):
    return jax.shard_map(
        on_device,
        mesh=mesh,
        in_specs=(P("blk", None), P("blk", "ch"), P("ch", None), P("blk", None), P("blk", "ch")),
        out_specs=(P("blk", None), P("ch", None)),
        check_vma=False,
    )
```

profile of v0, /device:TPU:0, one launch (start us, length us, event | category | flops | bytes accessed | tf_op | source)
XLA Modules:
  0.0 308.4 jit_solution(1734680084352292004)
XLA Ops:
  7.2 5.1 %collective-permute-start.7 = (bf16[256,128]{1,0:T(8,128)(2,1)}, bf16[256,128]{1,0:T(8,128)(2,1)S(1)}, u32[]{:S(2)}, u32[]{:S(2)}) collective-permute-start(bf16[256,128]{1,0:T(8,128)(2,1)} %param.9), channel_id=1, source_target_pairs={{8,0},{10,2},{12,4},{14,6},{16,8},{18,10},{20,12},{22,14},{24,16},... | collective-permute-start | bytes 196616 | tf_op jit(solution)/shard_map/ppermute | solution.py:12
  12.4 1.4 collective-permute-start.6
  13.7 1.4 collective-permute-start.5
  15.1 1.4 collective-permute-start.4
  16.6 1.6 collective-permute-start
  21.2 1.7 collective-permute-done
  23.5 6.5 %collective-permute-done.1 = bf16[256,128]{1,0:T(8,128)(2,1)S(1)} collective-permute-done((bf16[256,128]{1,0:T(8,128)(2,1)}, bf16[256,128]{1,0:T(8,128)(2,1)S(1)}, u32[]{:S(2)}, u32[]{:S(2)}) %collective-permute-start.1) | collective-permute-done | bytes 65568 | tf_op jit(solution)/shard_map/ppermute | solution.py:12
  30.7 6.5 %collective-permute-done.2 = bf16[256,128]{1,0:T(8,128)(2,1)S(1)} collective-permute-done((bf16[256,128]{1,0:T(8,128)(2,1)}, bf16[256,128]{1,0:T(8,128)(2,1)S(1)}, u32[]{:S(2)}, u32[]{:S(2)}) %collective-permute-start.2) | collective-permute-done | bytes 65568 | tf_op jit(solution)/shard_map/ppermute | solution.py:12
  37.2 1.5 collective-permute-start.3
  38.7 6.4 %collective-permute-done.3 = bf16[256,128]{1,0:T(8,128)(2,1)S(1)} collective-permute-done((bf16[256,128]{1,0:T(8,128)(2,1)S(1)}, bf16[256,128]{1,0:T(8,128)(2,1)S(1)}, u32[]{:S(2)}, u32[]{:S(2)}) %collective-permute-start.3) | collective-permute-done | bytes 65568 | tf_op jit(solution)/shard_map/ppermute | solution.py:12
  45.2 117.4 %while.23 = (s32[]{:T(128)}, f32[2304,128]{1,0:T(8,128)S(1)}, f32[256,128]{1,0:T(8,128)S(1)}, s32[20]{0:T(128)S(1)}, s32[256,20]{0,1:T(8,128)}, /*index=5*/s32[2...) while((s32[]{:T(128)}, f32[2304,128]{1,0:T(8,128)S(1)}, ...), condition=%wide.region_1.2_spmd.clone, body=%wide.region_0.1_spmd.clone.sunk | while | flops 312672256 | bytes 3772614 | solution.py:75
  54.4 1.3 select_add_fusion.2
  148.3 1.3 select_add_fusion.2
  163.8 2.0 collective-permute-start.15
  165.8 1.5 collective-permute-start.12
  167.5 1.6 collective-permute-done.8
  169.1 2.6 collective-permute-start.11
  172.0 1.8 collective-permute-start.10
  174.5 2.0 collective-permute-start.9
  177.6 3.0 collective-permute-done.9
  180.6 2.1 fusion.13
  182.7 97.4 %all-reduce.5.cloned.1.call-done = f32[128,256]{0,1:T(8,128)} async-done(((f32[128,256]{0,1:T(8,128)}), f32[128,256]{0,1:T(8,128)}) %all-reduce.5.cloned.1.call-update) | async-done | bytes 131088 | tf_op jit(solution)/shard_map/psum | solution.py:99
  281.8 18.2 %all-reduce.3.cloned.1.call-done = f32[256,128]{1,0:T(8,128)} async-done(((f32[256,128]{1,0:T(8,128)}), f32[256,128]{1,0:T(8,128)}) %all-reduce.3.cloned.1.call-update) | async-done | bytes 131088 | tf_op jit(solution)/shard_map/psum | solution.py:105
  299.9 1.6 copy.32
  (130 shorter events, 84.8 us)
Async XLA Ops:
  7.2 30.0 %copy-start = (bf16[256,128]{1,0:T(8,128)(2,1)S(1)}, bf16[256,128]{1,0:T(8,128)(2,1)}, u32[]{:S(2)}) copy-start(bf16[256,128]{1,0:T(8,128)(2,1)} %param.9) | copy-start | bytes 196612
  7.2 38.1 %copy-start.3 = (s32[256,128]{1,0:T(8,128)S(1)}, s32[256,128]{1,0:T(8,128)}, u32[]{:S(2)}) copy-start(s32[256,128]{1,0:T(8,128)} %param.13) | copy-start | bytes 393220
  7.2 272.9 %all-reduce.5.cloned.1.call-start = ((), (), s32[]{:S(2)}) async-start(), calls=%async_computation.1 | async-start | bytes 262144 | tf_op jit(solution)/shard_map/psum | solution.py:99
  7.2 38.0 %collective-permute-start.7 = (bf16[256,128]{1,0:T(8,128)(2,1)}, bf16[256,128]{1,0:T(8,128)(2,1)S(1)}, u32[]{:S(2)}, u32[]{:S(2)}) collective-permute-start(bf16[256,128]{1,0:T(8,128)(2,1)} %param.9), channel_id=1, source_target_pairs={{8,0},{10,2},{12,4},{14,6},{16,8},{18,10},{20,12},{22,14},{24,16},... | collective-permute-start | bytes 196616 | tf_op jit(solution)/shard_map/ppermute | solution.py:12
  12.4 32.8 %collective-permute-start.6 = (bf16[256,128]{1,0:T(8,128)(2,1)}, bf16[256,128]{1,0:T(8,128)(2,1)S(1)}, u32[]{:S(2)}, u32[]{:S(2)}) collective-permute-start(bf16[256,128]{1,0:T(8,128)(2,1)} %param.9), channel_id=1, source_target_pairs={{6,0},{8,2},{10,4},{12,6},{14,8},{16,10},{18,12},{20,14},{22,16},{... | collective-permute-start | bytes 196616 | tf_op jit(solution)/shard_map/ppermute | solution.py:12
  13.7 31.4 %collective-permute-start.5 = (bf16[256,128]{1,0:T(8,128)(2,1)}, bf16[256,128]{1,0:T(8,128)(2,1)S(1)}, u32[]{:S(2)}, u32[]{:S(2)}) collective-permute-start(bf16[256,128]{1,0:T(8,128)(2,1)} %param.9), channel_id=1, source_target_pairs={{4,0},{6,2},{8,4},{10,6},{12,8},{14,10},{16,12},{18,14},{20,16},{2... | collective-permute-start | bytes 196616 | tf_op jit(solution)/shard_map/ppermute | solution.py:12
  15.1 30.0 %collective-permute-start.4 = (bf16[256,128]{1,0:T(8,128)(2,1)}, bf16[256,128]{1,0:T(8,128)(2,1)S(1)}, u32[]{:S(2)}, u32[]{:S(2)}) collective-permute-start(bf16[256,128]{1,0:T(8,128)(2,1)} %param.9), channel_id=1, source_target_pairs={{2,0},{4,2},{6,4},{8,6},{10,8},{12,10},{14,12},{16,14},{18,16},{20... | collective-permute-start | bytes 196616 | tf_op jit(solution)/shard_map/ppermute | solution.py:12
  16.6 6.3 %collective-permute-start = (bf16[256,128]{1,0:T(8,128)(2,1)}, bf16[256,128]{1,0:T(8,128)(2,1)S(1)}, u32[]{:S(2)}, u32[]{:S(2)}) collective-permute-start(bf16[256,128]{1,0:T(8,128)(2,1)} %param.9), channel_id=1, source_target_pairs={{24,0},{26,2},{28,4},{30,6},{0,8},{2,10},{4,12},{6,14},{8,16},{10,... | collective-permute-start | bytes 196616 | tf_op jit(solution)/shard_map/ppermute | solution.py:12
  22.9 7.2 %collective-permute-start.1 = (bf16[256,128]{1,0:T(8,128)(2,1)}, bf16[256,128]{1,0:T(8,128)(2,1)S(1)}, u32[]{:S(2)}, u32[]{:S(2)}) collective-permute-start(bf16[256,128]{1,0:T(8,128)(2,1)} %param.9), channel_id=1, source_target_pairs={{26,0},{28,2},{30,4},{0,6},{2,8},{4,10},{6,12},{8,14},{10,16},{12,... | collective-permute-start | bytes 196616 | tf_op jit(solution)/shard_map/ppermute | solution.py:12
  30.0 7.2 %collective-permute-start.2 = (bf16[256,128]{1,0:T(8,128)(2,1)}, bf16[256,128]{1,0:T(8,128)(2,1)S(1)}, u32[]{:S(2)}, u32[]{:S(2)}) collective-permute-start(bf16[256,128]{1,0:T(8,128)(2,1)} %param.9), channel_id=1, source_target_pairs={{28,0},{30,2},{0,4},{2,6},{4,8},{6,10},{8,12},{10,14},{12,16},{14,... | collective-permute-start | bytes 196616 | tf_op jit(solution)/shard_map/ppermute | solution.py:12
  37.2 7.9 %collective-permute-start.3 = (bf16[256,128]{1,0:T(8,128)(2,1)S(1)}, bf16[256,128]{1,0:T(8,128)(2,1)S(1)}, u32[]{:S(2)}, u32[]{:S(2)}) collective-permute-start(bf16[256,128]{1,0:T(8,128)(2,1)S(1)} %copy-done), channel_id=1, source_target_pairs={{30,0},{0,2},{2,4},{4,6},{6,8},{8,10},{10,12},{12,14},{14,16},{16,... | collective-permute-start | bytes 196616 | tf_op jit(solution)/shard_map/ppermute | solution.py:12
  45.2 117.4 %copy-start.1 = (bf16[128,256]{1,0:T(8,128)(2,1)S(1)}, bf16[128,256]{1,0:T(8,128)(2,1)}, u32[]{:S(2)}) copy-start(bf16[128,256]{1,0:T(8,128)(2,1)} %param.11) | copy-start | bytes 196612
  163.8 5.3 %collective-permute-start.8 = (f32[256,128]{1,0:T(8,128)S(1)}, f32[256,128]{1,0:T(8,128)S(1)}, u32[]{:S(2)}, u32[]{:S(2)}) collective-permute-start(f32[256,128]{1,0:T(8,128)S(1)} %get-tuple-element.176), channel_id=1, source_target_pairs={{8,0},{10,2},{12,4},{14,6},{16,8},{18,10},{20,12},{22,14},{24,16},... | collective-permute-start | bytes 393224 | tf_op jit(solution)/shard_map/ppermute | solution.py:12
  163.8 8.2 %collective-permute-start.15 = (f32[256,128]{1,0:T(8,128)S(1)}, f32[256,128]{1,0:T(8,128)S(1)}, u32[]{:S(2)}, u32[]{:S(2)}) collective-permute-start(f32[256,128]{1,0:T(8,128)S(1)} %get-tuple-element.177), channel_id=1, source_target_pairs={{24,0},{26,2},{28,4},{30,6},{0,8},{2,10},{4,12},{6,14},{8,16},{10,... | collective-permute-start | bytes 393224 | tf_op jit(solution)/shard_map/ppermute | solution.py:12
  165.8 8.0 %collective-permute-start.14 = (f32[256,128]{1,0:T(8,128)S(1)}, f32[256,128]{1,0:T(8,128)S(1)}, u32[]{:S(2)}, u32[]{:S(2)}) collective-permute-start(f32[256,128]{1,0:T(8,128)S(1)} %get-tuple-element.178), channel_id=1, source_target_pairs={{26,0},{28,2},{30,4},{0,6},{2,8},{4,10},{6,12},{8,14},{10,16},{12,... | collective-permute-start | bytes 393224 | tf_op jit(solution)/shard_map/ppermute | solution.py:12
  165.8 11.7 %collective-permute-start.13 = (f32[256,128]{1,0:T(8,128)}, f32[256,128]{1,0:T(8,128)}, u32[]{:S(2)}, u32[]{:S(2)}) collective-permute-start(f32[256,128]{1,0:T(8,128)} %get-tuple-element.179), channel_id=1, source_target_pairs={{28,0},{30,2},{0,4},{2,6},{4,8},{6,10},{8,12},{10,14},{12,16},{14,... | collective-permute-start | bytes 393224 | tf_op jit(solution)/shard_map/ppermute | solution.py:12
  165.8 11.7 %collective-permute-start.12 = (f32[256,128]{1,0:T(8,128)}, f32[256,128]{1,0:T(8,128)}, u32[]{:S(2)}, u32[]{:S(2)}) collective-permute-start(f32[256,128]{1,0:T(8,128)} %get-tuple-element.180), channel_id=1, source_target_pairs={{30,0},{0,2},{2,4},{4,6},{6,8},{8,10},{10,12},{12,14},{14,16},{16,... | collective-permute-start | bytes 393224 | tf_op jit(solution)/shard_map/ppermute | solution.py:12
  169.1 8.4 %collective-permute-start.11 = (f32[256,128]{1,0:T(8,128)}, f32[256,128]{1,0:T(8,128)}, u32[]{:S(2)}, u32[]{:S(2)}) collective-permute-start(f32[256,128]{1,0:T(8,128)} %get-tuple-element.181), channel_id=1, source_target_pairs={{2,0},{4,2},{6,4},{8,6},{10,8},{12,10},{14,12},{16,14},{18,16},{20... | collective-permute-start | bytes 393224 | tf_op jit(solution)/shard_map/ppermute | solution.py:12
  172.0 5.6 %collective-permute-start.10 = (f32[256,128]{1,0:T(8,128)}, f32[256,128]{1,0:T(8,128)}, u32[]{:S(2)}, u32[]{:S(2)}) collective-permute-start(f32[256,128]{1,0:T(8,128)} %get-tuple-element.182), channel_id=1, source_target_pairs={{4,0},{6,2},{8,4},{10,6},{12,8},{14,10},{16,12},{18,14},{20,16},{2... | collective-permute-start | bytes 393224 | tf_op jit(solution)/shard_map/ppermute | solution.py:12
  173.8 0.7 copy-start.2
  174.5 6.2 %collective-permute-start.9 = (f32[256,128]{1,0:T(8,128)}, f32[256,128]{1,0:T(8,128)}, u32[]{:S(2)}, u32[]{:S(2)}) collective-permute-start(f32[256,128]{1,0:T(8,128)} %get-tuple-element.183), channel_id=1, source_target_pairs={{6,0},{8,2},{10,4},{12,6},{14,8},{16,10},{18,12},{20,14},{22,16},{... | collective-permute-start | bytes 393224 | tf_op jit(solution)/shard_map/ppermute | solution.py:12
  177.5 122.5 %all-reduce.3.cloned.1.call-start = ((), (), s32[]{:S(2)}) async-start(), calls=%async_computation | async-start | bytes 262144 | tf_op jit(solution)/shard_map/psum | solution.py:105
Sparse Core Ops, SparseCore 0:
  177.6 102.4 all-reduce.4
  283.0 16.9 all-reduce.2
where the time goes:
time: 310 us; the launch traced here: 308 us
  waiting for transfers between devices  142 us (46%)
  matrix products  56 us (18%)
  loops' own time  39.5 us (13%)
  local copies, waits for them, and re-layouts  31 us (10%)
  starting transfers between devices  23.6 us (8%)
  between operations  14.2 us (5%)
    psum x1, waiting for transfers between devices, on_device(): weight_grad = lax.psum(weight_terms, 'blk') * total_points ** (-0.5)  97.4 us
    another operation x1, loops' own time, point_block(): lax.scan(per_edge, (window_acc, start_total), edge_order)  39.5 us
    dot_general x20, matrix products, per_edge(): jnp.dot(picked, w_nbr_t, preferred_element_type=jnp.float32)  26.6 us
    ppermute x16, waiting for transfers between devices, shifted(): return lax.ppermute(block, axis, route)  26.1 us
    dot_general x20, matrix products, per_edge(): lax.dot_general(one_hot, edge_grad, (((0,), (0,)), ((), ())), preferred_e...  25.4 us
    ppermute x16, starting transfers between devices, shifted(): return lax.ppermute(block, axis, route)  23.5 us
    psum x1, waiting for transfers between devices, on_device(): feature_grad = lax.psum(summed, 'ch')  18.2 us
    dynamic_slice x20, local copies, waits for them, and re-layouts, per_edge(): slot_col = lax.dynamic_slice_in_dim(slot_rows, edge_index, 1, 1)  14.1 us
  transfers between devices with their start and end apart: 18, of which 9 were waited for; matrix products, arithmetic and copies ran while one was open for 3% of the time, Pallas kernels for 0%

commit v1 on v0

--- a/solution.py
+++ b/solution.py
@@ -96,7 +96,11 @@
     )
     weight_terms = jnp.concatenate([own_part, nbr_total - own_part], axis=1)
     total_points = points * lax.axis_size("blk")
-    weight_grad = lax.psum(weight_terms, "blk") * total_points ** (-0.5)
+
+    def match_ports_now(local_x):
+        return jax.lax.all_gather(local_x, "blk").sum(axis=0)
+
+    weight_grad = match_ports_now(weight_terms) * total_points ** (-0.5)
     self_grad = jnp.dot(grad_sum, w_diff, preferred_element_type=jnp.float32)
     contrib = jnp.dot(gathered, w_nbr, preferred_element_type=jnp.float32)
     contrib = contrib.reshape(2 * REACH + 1, points, in_width)

time: 310 us -> 231 us (0.75)
  waiting for transfers between devices: 142 us -> 60.2 us
    psum x1 -> x0, waiting for transfers between devices: 97.4 us -> none  [on_device(): weight_grad = lax.psum(weight_terms, 'blk') * total_points ** (-0.5)]
    all_gather x0 -> x1, waiting for transfers between devices: none -> 44 us  [match_ports_now(): return jax.lax.all_gather(local_x, 'blk').sum(axis=0)]
    psum x1, waiting for transfers between devices: 18.2 us -> 0.01 us  [on_device(): feature_grad = lax.psum(summed, 'ch')]
    ppermute x16, waiting for transfers between devices: 26.1 us -> 16.2 us  [shifted(): return lax.ppermute(block, axis, route)]
  transfers between devices with their start and end apart: 18 -> 18, of which waited for: 9 -> 8; matrix products, arithmetic and copies ran while one was open for 3% -> 3% of each run, Pallas kernels for 0% -> 0%
where the time goes in v1:
time: 231 us; the launch traced here: 229 us
  waiting for transfers between devices  60.2 us (26%)
  matrix products  54.7 us (24%)
  loops' own time  39.5 us (17%)
  local copies, waits for them, and re-layouts  31.4 us (14%)
  starting transfers between devices  25.2 us (11%)
  between operations  15.7 us (7%)
    all_gather x1, waiting for transfers between devices, match_ports_now(): return jax.lax.all_gather(local_x, 'blk').sum(axis=0)  44 us
    another operation x1, loops' own time, point_block(): lax.scan(per_edge, (window_acc, start_total), edge_order)  39.5 us
    dot_general x20, matrix products, per_edge(): jnp.dot(picked, w_nbr_t, preferred_element_type=jnp.float32)  26.6 us
    dot_general x20, matrix products, per_edge(): lax.dot_general(one_hot, edge_grad, (((0,), (0,)), ((), ())), preferred_e...  25.4 us
    ppermute x16, starting transfers between devices, shifted(): return lax.ppermute(block, axis, route)  25.1 us
    ppermute x16, waiting for transfers between devices, shifted(): return lax.ppermute(block, axis, route)  16.2 us
    dynamic_slice x20, local copies, waits for them, and re-layouts, per_edge(): slot_col = lax.dynamic_slice_in_dim(slot_rows, edge_index, 1, 1)  14.1 us
    dynamic_slice x20, local copies, waits for them, and re-layouts, point_block(): lax.scan(per_edge, (window_acc, start_total), edge_order)  11.7 us
  transfers between devices with their start and end apart: 18, of which 8 were waited for; matrix products, arithmetic and copies ran while one was open for 3% of the time, Pallas kernels for 0%

profile of v1, /device:TPU:0, one launch (start us, length us, event | category | flops | bytes accessed | tf_op | source)
XLA Modules:
  0.0 228.7 jit_solution(6072720790514264453)
XLA Ops:
  8.1 3.1 %collective-permute-start = (bf16[256,128]{1,0:T(8,128)(2,1)}, bf16[256,128]{1,0:T(8,128)(2,1)S(1)}, u32[]{:S(2)}, u32[]{:S(2)}) collective-permute-start(bf16[256,128]{1,0:T(8,128)(2,1)} %param.9), channel_id=1, source_target_pairs={{24,0},{26,2},{28,4},{30,6},{0,8},{2,10},{4,12},{6,14},{8,16},{10,... | collective-permute-start | bytes 196616 | tf_op jit(solution)/shard_map/ppermute | solution.py:12
  11.2 2.4 %collective-permute-start.1 = (bf16[256,128]{1,0:T(8,128)(2,1)}, bf16[256,128]{1,0:T(8,128)(2,1)S(1)}, u32[]{:S(2)}, u32[]{:S(2)}) collective-permute-start(bf16[256,128]{1,0:T(8,128)(2,1)} %param.9), channel_id=1, source_target_pairs={{26,0},{28,2},{30,4},{0,6},{2,8},{4,10},{6,12},{8,14},{10,16},{12,... | collective-permute-start | bytes 196616 | tf_op jit(solution)/shard_map/ppermute | solution.py:12
  13.6 1.5 collective-permute-start.2
  15.7 5.0 %collective-permute-start.4 = (bf16[256,128]{1,0:T(8,128)(2,1)}, bf16[256,128]{1,0:T(8,128)(2,1)S(1)}, u32[]{:S(2)}, u32[]{:S(2)}) collective-permute-start(bf16[256,128]{1,0:T(8,128)(2,1)} %param.9), channel_id=1, source_target_pairs={{2,0},{4,2},{6,4},{8,6},{10,8},{12,10},{14,12},{16,14},{18,16},{20... | collective-permute-start | bytes 196616 | tf_op jit(solution)/shard_map/ppermute | solution.py:12
  25.4 2.9 %collective-permute-done.5 = bf16[256,128]{1,0:T(8,128)(2,1)S(1)} collective-permute-done((bf16[256,128]{1,0:T(8,128)(2,1)}, bf16[256,128]{1,0:T(8,128)(2,1)S(1)}, u32[]{:S(2)}, u32[]{:S(2)}) %collective-permute-start.5) | collective-permute-done | bytes 65568 | tf_op jit(solution)/shard_map/ppermute | solution.py:12
  28.4 1.5 collective-permute-done.6
  29.9 117.3 %while.23 = (s32[]{:T(128)}, f32[2304,128]{1,0:T(8,128)S(1)}, f32[256,128]{1,0:T(8,128)S(1)}, s32[20]{0:T(128)S(1)}, s32[256,20]{0,1:T(8,128)}, /*index=5*/s32[2...) while((s32[]{:T(128)}, f32[2304,128]{1,0:T(8,128)S(1)}, ...), condition=%wide.region_1.2_spmd.clone, body=%wide.region_0.1_spmd.clone.sunk | while | flops 312672256 | bytes 3772606 | solution.py:75
  44.8 1.3 select_add_fusion.2
  50.7 1.3 select_add_fusion.2
  62.4 1.3 select_add_fusion.2
  68.3 1.3 select_add_fusion.2
  85.9 1.3 select_add_fusion.2
  103.5 1.3 select_add_fusion.2
  121.1 1.3 select_add_fusion.2
  138.7 1.3 select_add_fusion.2
  148.9 4.1 %collective-permute-start.10 = (f32[256,128]{1,0:T(8,128)S(1)}, f32[256,128]{1,0:T(8,128)S(1)}, u32[]{:S(2)}, u32[]{:S(2)}) collective-permute-start(f32[256,128]{1,0:T(8,128)S(1)} %get-tuple-element.192), channel_id=1, source_target_pairs={{4,0},{6,2},{8,4},{10,6},{12,8},{14,10},{16,12},{18,14},{20,16},{2... | collective-permute-start | bytes 393224 | tf_op jit(solution)/shard_map/ppermute | solution.py:12
  155.1 1.6 collective-permute-start.14
  157.6 1.8 collective-permute-done.11
  159.4 2.3 collective-permute-start.8
  161.7 3.3 %collective-permute-done.12 = f32[256,128]{1,0:T(8,128)S(1)} collective-permute-done((f32[256,128]{1,0:T(8,128)S(1)}, f32[256,128]{1,0:T(8,128)S(1)}, u32[]{:S(2)}, u32[]{:S(2)}) %collective-permute-start.12) | collective-permute-done | bytes 131104 | tf_op jit(solution)/shard_map/ppermute | solution.py:12
  166.4 5.2 %collective-permute-done.9 = f32[256,128]{1,0:T(8,128)S(1)} collective-permute-done((f32[256,128]{1,0:T(8,128)S(1)}, f32[256,128]{1,0:T(8,128)S(1)}, u32[]{:S(2)}, u32[]{:S(2)}) %collective-permute-start.9) | collective-permute-done | bytes 131104 | tf_op jit(solution)/shard_map/ppermute | solution.py:12
  172.5 44.0 %all-gather.3.cloned.1.call-done = f32[2048,256]{0,1:T(8,128)} async-done(((f32[128,256]{0,1:T(8,128)}), f32[2048,256]{0,1:T(8,128)}) %all-gather.3.cloned.1.call-update) | async-done | bytes 2097168 | tf_op jit(solution)/shard_map/all_gather | solution.py:101
  216.6 2.0 copy.16
  219.7 1.6 copy.35
  (130 shorter events, 80.5 us)
Async XLA Ops:
  8.0 16.5 %copy-start = (bf16[256,128]{1,0:T(8,128)(2,1)S(1)}, bf16[256,128]{1,0:T(8,128)(2,1)}, u32[]{:S(2)}) copy-start(bf16[256,128]{1,0:T(8,128)(2,1)} %param.9) | copy-start | bytes 196612
  8.0 21.9 %copy-start.2 = (s32[256,128]{1,0:T(8,128)S(1)}, s32[256,128]{1,0:T(8,128)}, u32[]{:S(2)}) copy-start(s32[256,128]{1,0:T(8,128)} %param.13) | copy-start | bytes 393220
  8.0 208.5 %all-gather.3.cloned.1.call-start = ((), (), s32[]{:S(2)}) async-start(), calls=%async_computation.1 | async-start | bytes 2228224 | tf_op jit(solution)/shard_map/all_gather | solution.py:101
  8.1 15.7 %collective-permute-start = (bf16[256,128]{1,0:T(8,128)(2,1)}, bf16[256,128]{1,0:T(8,128)(2,1)S(1)}, u32[]{:S(2)}, u32[]{:S(2)}) collective-permute-start(bf16[256,128]{1,0:T(8,128)(2,1)} %param.9), channel_id=1, source_target_pairs={{24,0},{26,2},{28,4},{30,6},{0,8},{2,10},{4,12},{6,14},{8,16},{10,... | collective-permute-start | bytes 196616 | tf_op jit(solution)/shard_map/ppermute | solution.py:12
  11.2 13.2 %collective-permute-start.1 = (bf16[256,128]{1,0:T(8,128)(2,1)}, bf16[256,128]{1,0:T(8,128)(2,1)S(1)}, u32[]{:S(2)}, u32[]{:S(2)}) collective-permute-start(bf16[256,128]{1,0:T(8,128)(2,1)} %param.9), channel_id=1, source_target_pairs={{26,0},{28,2},{30,4},{0,6},{2,8},{4,10},{6,12},{8,14},{10,16},{12,... | collective-permute-start | bytes 196616 | tf_op jit(solution)/shard_map/ppermute | solution.py:12
  13.6 10.9 %collective-permute-start.2 = (bf16[256,128]{1,0:T(8,128)(2,1)}, bf16[256,128]{1,0:T(8,128)(2,1)S(1)}, u32[]{:S(2)}, u32[]{:S(2)}) collective-permute-start(bf16[256,128]{1,0:T(8,128)(2,1)} %param.9), channel_id=1, source_target_pairs={{28,0},{30,2},{0,4},{2,6},{4,8},{6,10},{8,12},{10,14},{12,16},{14,... | collective-permute-start | bytes 196616 | tf_op jit(solution)/shard_map/ppermute | solution.py:12
  15.1 10.2 %collective-permute-start.3 = (bf16[256,128]{1,0:T(8,128)(2,1)}, bf16[256,128]{1,0:T(8,128)(2,1)S(1)}, u32[]{:S(2)}, u32[]{:S(2)}) collective-permute-start(bf16[256,128]{1,0:T(8,128)(2,1)} %param.9), channel_id=1, source_target_pairs={{30,0},{0,2},{2,4},{4,6},{6,8},{8,10},{10,12},{12,14},{14,16},{16,... | collective-permute-start | bytes 196616 | tf_op jit(solution)/shard_map/ppermute | solution.py:12
  15.7 9.6 %collective-permute-start.4 = (bf16[256,128]{1,0:T(8,128)(2,1)}, bf16[256,128]{1,0:T(8,128)(2,1)S(1)}, u32[]{:S(2)}, u32[]{:S(2)}) collective-permute-start(bf16[256,128]{1,0:T(8,128)(2,1)} %param.9), channel_id=1, source_target_pairs={{2,0},{4,2},{6,4},{8,6},{10,8},{12,10},{14,12},{16,14},{18,16},{20... | collective-permute-start | bytes 196616 | tf_op jit(solution)/shard_map/ppermute | solution.py:12
  23.8 4.5 %collective-permute-start.5 = (bf16[256,128]{1,0:T(8,128)(2,1)}, bf16[256,128]{1,0:T(8,128)(2,1)S(1)}, u32[]{:S(2)}, u32[]{:S(2)}) collective-permute-start(bf16[256,128]{1,0:T(8,128)(2,1)} %param.9), channel_id=1, source_target_pairs={{4,0},{6,2},{8,4},{10,6},{12,8},{14,10},{16,12},{18,14},{20,16},{2... | collective-permute-start | bytes 196616 | tf_op jit(solution)/shard_map/ppermute | solution.py:12
  24.4 5.4 %collective-permute-start.6 = (bf16[256,128]{1,0:T(8,128)(2,1)}, bf16[256,128]{1,0:T(8,128)(2,1)S(1)}, u32[]{:S(2)}, u32[]{:S(2)}) collective-permute-start(bf16[256,128]{1,0:T(8,128)(2,1)} %param.9), channel_id=1, source_target_pairs={{6,0},{8,2},{10,4},{12,6},{14,8},{16,10},{18,12},{20,14},{22,16},{... | collective-permute-start | bytes 196616 | tf_op jit(solution)/shard_map/ppermute | solution.py:12
  24.5 5.3 %collective-permute-start.7 = (bf16[256,128]{1,0:T(8,128)(2,1)S(1)}, bf16[256,128]{1,0:T(8,128)(2,1)S(1)}, u32[]{:S(2)}, u32[]{:S(2)}) collective-permute-start(bf16[256,128]{1,0:T(8,128)(2,1)S(1)} %copy-done), channel_id=1, source_target_pairs={{8,0},{10,2},{12,4},{14,6},{16,8},{18,10},{20,12},{22,14},{24,16},... | collective-permute-start | bytes 196616 | tf_op jit(solution)/shard_map/ppermute | solution.py:12
  147.4 1.1 copy-start.1
  148.4 71.2 %all-reduce.2.cloned.1.call-start = ((), (), s32[]{:S(2)}) async-start(), calls=%async_computation | async-start | bytes 262144 | tf_op jit(solution)/shard_map/psum | solution.py:109
  148.9 7.8 %collective-permute-start.10 = (f32[256,128]{1,0:T(8,128)S(1)}, f32[256,128]{1,0:T(8,128)S(1)}, u32[]{:S(2)}, u32[]{:S(2)}) collective-permute-start(f32[256,128]{1,0:T(8,128)S(1)} %get-tuple-element.192), channel_id=1, source_target_pairs={{4,0},{6,2},{8,4},{10,6},{12,8},{14,10},{16,12},{18,14},{20,16},{2... | collective-permute-start | bytes 393224 | tf_op jit(solution)/shard_map/ppermute | solution.py:12
  153.0 6.4 %collective-permute-start.11 = (f32[256,128]{1,0:T(8,128)S(1)}, f32[256,128]{1,0:T(8,128)S(1)}, u32[]{:S(2)}, u32[]{:S(2)}) collective-permute-start(f32[256,128]{1,0:T(8,128)S(1)} %get-tuple-element.191), channel_id=1, source_target_pairs={{2,0},{4,2},{6,4},{8,6},{10,8},{12,10},{14,12},{16,14},{18,16},{20... | collective-permute-start | bytes 393224 | tf_op jit(solution)/shard_map/ppermute | solution.py:12
  154.3 10.7 %collective-permute-start.12 = (f32[256,128]{1,0:T(8,128)S(1)}, f32[256,128]{1,0:T(8,128)S(1)}, u32[]{:S(2)}, u32[]{:S(2)}) collective-permute-start(f32[256,128]{1,0:T(8,128)S(1)} %get-tuple-element.190), channel_id=1, source_target_pairs={{30,0},{0,2},{2,4},{4,6},{6,8},{8,10},{10,12},{12,14},{14,16},{16,... | collective-permute-start | bytes 393224 | tf_op jit(solution)/shard_map/ppermute | solution.py:12
  155.1 9.9 %collective-permute-start.13 = (f32[256,128]{1,0:T(8,128)S(1)}, f32[256,128]{1,0:T(8,128)S(1)}, u32[]{:S(2)}, u32[]{:S(2)}) collective-permute-start(f32[256,128]{1,0:T(8,128)S(1)} %get-tuple-element.189), channel_id=1, source_target_pairs={{28,0},{30,2},{0,4},{2,6},{4,8},{6,10},{8,12},{10,14},{12,16},{14,... | collective-permute-start | bytes 393224 | tf_op jit(solution)/shard_map/ppermute | solution.py:12
  155.1 10.4 %collective-permute-start.14 = (f32[256,128]{1,0:T(8,128)S(1)}, f32[256,128]{1,0:T(8,128)S(1)}, u32[]{:S(2)}, u32[]{:S(2)}) collective-permute-start(f32[256,128]{1,0:T(8,128)S(1)} %get-tuple-element.188), channel_id=1, source_target_pairs={{26,0},{28,2},{30,4},{0,6},{2,8},{4,10},{6,12},{8,14},{10,16},{12,... | collective-permute-start | bytes 393224 | tf_op jit(solution)/shard_map/ppermute | solution.py:12
  156.7 8.8 %collective-permute-start.15 = (f32[256,128]{1,0:T(8,128)S(1)}, f32[256,128]{1,0:T(8,128)S(1)}, u32[]{:S(2)}, u32[]{:S(2)}) collective-permute-start(f32[256,128]{1,0:T(8,128)S(1)} %get-tuple-element.187), channel_id=1, source_target_pairs={{24,0},{26,2},{28,4},{30,6},{0,8},{2,10},{4,12},{6,14},{8,16},{10,... | collective-permute-start | bytes 393224 | tf_op jit(solution)/shard_map/ppermute | solution.py:12
  159.4 7.0 %collective-permute-start.8 = (f32[256,128]{1,0:T(8,128)S(1)}, f32[256,128]{1,0:T(8,128)S(1)}, u32[]{:S(2)}, u32[]{:S(2)}) collective-permute-start(f32[256,128]{1,0:T(8,128)S(1)} %get-tuple-element.186), channel_id=1, source_target_pairs={{8,0},{10,2},{12,4},{14,6},{16,8},{18,10},{20,12},{22,14},{24,16},... | collective-permute-start | bytes 393224 | tf_op jit(solution)/shard_map/ppermute | solution.py:12
  165.0 6.7 %collective-permute-start.9 = (f32[256,128]{1,0:T(8,128)S(1)}, f32[256,128]{1,0:T(8,128)S(1)}, u32[]{:S(2)}, u32[]{:S(2)}) collective-permute-start(f32[256,128]{1,0:T(8,128)S(1)} %get-tuple-element.193), channel_id=1, source_target_pairs={{6,0},{8,2},{10,4},{12,6},{14,8},{16,10},{18,12},{20,14},{22,16},{... | collective-permute-start | bytes 393224 | tf_op jit(solution)/shard_map/ppermute | solution.py:12
Sparse Core Ops, SparseCore 0:
  148.6 67.9 all-gather.2
Sparse Core Ops, SparseCore 1:
  172.6 16.7 all-reduce.1
